TPU v7x, 32 devices: a whole 2x2x4 slice. The times are simulated.
32 devices in a mesh: feat: 8 (over z, y), samp: 4 (over x, core).
Axes of the slice: x: 2, y: 2, z: 4, core: 2. Of those that a mesh axis runs over, the one named last changes fastest.
Arguments:
- design: bfloat16 [14336, 8192], P('samp', 'feat'), may hold values from -0.0625 to 0.0625
- targets: bfloat16 [14336, 128], P('samp'), may hold values from -26 to 26
- warm_start: float32 [8192, 128], P('feat'), may hold values from -0.6 to 0.6
- active_mask: int32 [2, 8192], P(None, 'feat'), may hold values 0 or 1
- penalty_index: int32 [1], replicated, may hold values from 0 to 7
Outputs:
- coefficients: float32 [8192, 128], P('feat')
- correlations: float32 [3, 8192], P(None, 'feat')
- relative_gaps: float32 [3], replicated
- pruned_counts: float32 [2], replicated
All inputs are finite; a program needn't handle non-finite values. No bound on the sum of `active_mask` on one device may be relied on, other than what follows from the above.
Results may differ from a plain program's by a relative error of at most 0.0024.
The roundings to bfloat16 on the way count: a program that leaves them out, or rounds other values in their place, can miss the bound.
Values may be sent and summed in bfloat16 or wider, within the bound.
A program may use at most 64 MiB of HBM per device.

v0:
```python
import jax
import jax.numpy as jnp
from jax import lax
from jax.sharding import PartitionSpec as P

ITERS = 2


def group_norms(matrix):
    return jnp.sqrt(jnp.sum(matrix * matrix, axis=1))


def transpose_product(design, right_side):
    return lax.dot_general(
        design, right_side, (((0,), (0,)), ((), ())), preferred_element_type=jnp.float32
    )


def local(design, targets, warm_start, active_mask, penalty_index):
    row_count, col_count = design.shape
    feat_size = lax.axis_size("feat")
    feat_slot = lax.axis_index("feat")
    block_rows = row_count // feat_size
    samp_first = (lax.axis_index("samp") == 0).astype(jnp.float32)
    corr_local = transpose_product(design, targets)
    squares_local = jnp.sum(jnp.square(design.astype(jnp.float32)), axis=0)
    corr_y, column_squares = lax.psum((corr_local, squares_local), "samp")
    penalty_max = lax.pmax(jnp.max(group_norms(corr_y)), "feat")
    penalty = penalty_max / (8.0 + 4.0 * penalty_index[0].astype(jnp.float32))
    step_sizes = 0.5 / (1.0 + column_squares)
    current = warm_start
    correlations = []
    relative_gaps = []
    pruned_counts = []
    own_targets = lax.dynamic_slice_in_dim(targets, feat_slot * block_rows, block_rows, 0)
    for iteration in range(ITERS + 1):
        current_half = current.astype(jnp.bfloat16)
        fitted_part = jnp.dot(design, current_half, preferred_element_type=jnp.float32)
        fitted = lax.psum(fitted_part, "feat")
        residual_all = (targets.astype(jnp.float32) - fitted).astype(jnp.bfloat16)
        residual = lax.dynamic_slice_in_dim(residual_all, feat_slot * block_rows, block_rows, 0)
        grad_local = transpose_product(design, residual_all)
        resid_float = residual.astype(jnp.float32)
        rr_local = jnp.sum(resid_float * resid_float)
        ry_local = jnp.sum(resid_float * own_targets.astype(jnp.float32))
        bn_local = samp_first * jnp.sum(group_norms(current))
        if iteration < ITERS:
            keep = active_mask[iteration].astype(jnp.float32)
            pruned_local = samp_first * jnp.sum(1.0 - keep)
        else:
            pruned_local = jnp.zeros((), jnp.float32)
        gradient = lax.psum(grad_local, "samp")
        grad_norms = group_norms(gradient)
        local_max = jnp.max(grad_norms)
        grad_top = lax.pmax(local_max, "feat")
        rr_sum, ry_sum, bn_sum, pruned_sum = lax.psum(
            (rr_local, ry_local, bn_local, pruned_local), ("feat", "samp")
        )
        scale = jnp.maximum(penalty, grad_top)
        correlations.append(grad_norms / scale)
        primal = 0.5 * rr_sum + penalty * bn_sum
        ratio = penalty / scale
        dual = ratio * ry_sum - 0.5 * ratio * ratio * rr_sum
        relative_gaps.append((primal - dual) / (primal + 1.0))
        if iteration < ITERS:
            pruned_counts.append(pruned_sum)
            moved = current + step_sizes[:, None] * gradient
            moved_norms = group_norms(moved)
            cutoff = step_sizes * penalty
            factor = jnp.maximum(moved_norms - cutoff, 0.0) / jnp.maximum(moved_norms, cutoff)
            current = (keep * factor)[:, None] * moved
    return (current, jnp.stack(correlations), jnp.stack(relative_gaps), jnp.stack(pruned_counts))


def solution(mesh):
    placed = (P("samp", "feat"), P("samp", None), P("feat", None), P(None, "feat"), P())
    return jax.shard_map(
        local,
        mesh=mesh,
        in_specs=placed,
        out_specs=(P("feat", None), P(None, "feat"), P(), P()),
        check_vma=False,
    )
```

profile of v0, /device:TPU:0, one launch (start us, length us, event | category | flops | bytes accessed | tf_op | source)
XLA Modules:
  0.0 527.3 jit_solution(8647449387170644454)
XLA Ops:
  7.2 6.5 %fusion.5 = f32[3584,128]{1,0:T(8,128)} fusion(bf16[3584,1024]{1,0:T(8,128)(2,1)} %param.5, f32[1024,128]{1,0:T(8,128)} %param.7), kind=kOutput, calls=%fused_computation.33 | convolution fusion | flops 939655168 | bytes 9699328 | tf_op jit(solution)/shard_map/dot_general | solution.py:38
  13.8 6.0 %fusion.13 = f32[1024,128]{1,0:T(8,128)} fusion(bf16[3584,1024]{1,0:T(8,128)(2,1)} %param.5, bf16[3584,128]{1,0:T(8,128)(2,1)S(1)} %copy-done), kind=kOutput, calls=%fused_computation.61 | convolution fusion | flops 939524096 | bytes 8781824 | tf_op jit(solution)/shard_map/dot_general | solution.py:14
  19.8 92.7 %all-reduce.10.cloned.1.call-done = f32[3584,128]{1,0:T(8,128)} async-done(((f32[3584,128]{1,0:T(8,128)}), f32[3584,128]{1,0:T(8,128)}) %all-reduce.10.cloned.1.call-update) | async-done | bytes 1835024 | tf_op jit(solution)/shard_map/psum | solution.py:39
  112.5 1.7 fusion
  114.1 5.0 convolution_bitcast_fusion.4
  119.3 4.6 multiply_reduce_fusion
  125.5 7.1 %psum.133 = f32[1024]{0:T(1024)S(1)} all-reduce(f32[1024]{0:T(1024)S(1)} %multiply_reduce_fusion), channel_id=1, replica_groups=mesh['feat'=8,'samp'=4] {'samp'}, use_global_device_ids=true, to_apply=%region_1.0 | all-reduce | flops 1024 | bytes 8192 | tf_op jit(solution)/shard_map/psum | solution.py:27
  132.7 22.5 %all-reduce.20.cloned.1.call-done = (f32[1024,128]{0,1:T(8,128)}, f32[1024,128]{1,0:T(8,128)}) async-done(((f32[1024,128]{0,1:T(8,128)}, f32[1024,128]{1,0:T(8,128)}), (f32[1024,128]{0,1:T(8,128)}, f32[1024,128]{1,0:T(8,128)})) %all-reduce.20.cloned.1.call-update) | async-done | bytes 1048592 | tf_op jit(solution)/shard_map/psum | solution.py:52
  155.2 1.2 multiply_reduce_fusion.8
  157.1 22.0 %pmax.28 = f32[]{:T(128)} all-reduce(f32[]{:T(128)} %sqrt_reduce_fusion.3), channel_id=1, replica_groups=mesh['feat'=8,'samp'=4] {'feat'}, use_global_device_ids=true, to_apply=%region_8.0 | all-reduce | flops 1 | bytes 8 | tf_op jit(solution)/shard_map/pmax | solution.py:28
  179.7 1.3 multiply_reduce_fusion.9
  181.7 6.4 %convolution_bitcast_fusion.1 = f32[3584,128]{1,0:T(8,128)} fusion(bf16[3584,1024]{1,0:T(8,128)(2,1)} %param.5, f32[1024,128]{0,1:T(8,128)S(1)} %get-tuple-element.36, f32[1024]{0:T(1024)S(1)} %get-tuple-element.41), kind=kOutput, calls=%fused_computation.2 | convolution fusion | flops 939786240 | bytes 9703424 | tf_op jit(solution)/shard_map/dot_general | solution.py:38
  188.1 92.7 %all-reduce.12.cloned.1.call-done = f32[3584,128]{1,0:T(8,128)} async-done(((f32[3584,128]{1,0:T(8,128)}), f32[3584,128]{1,0:T(8,128)}) %all-reduce.12.cloned.1.call-update) | async-done | bytes 1835024 | tf_op jit(solution)/shard_map/psum | solution.py:39
  280.9 1.7 fusion.1
  282.6 5.0 convolution_bitcast_fusion.3
  287.8 32.8 %all-reduce.14.cloned.1.call-done = f32[1024,128]{0,1:T(8,128)} async-done(((f32[1024,128]{0,1:T(8,128)}), f32[1024,128]{0,1:T(8,128)}) %all-reduce.14.cloned.1.call-update) | async-done | bytes 524304 | tf_op jit(solution)/shard_map/psum | solution.py:52
  324.5 6.4 %convolution_bitcast_fusion = f32[3584,128]{1,0:T(8,128)} fusion(bf16[3584,1024]{1,0:T(8,128)(2,1)} %param.5, f32[1024,128]{0,1:T(8,128)S(1)} %get-tuple-element.34), kind=kOutput, calls=%fused_computation.1 | convolution fusion | flops 939655168 | bytes 9699328 | tf_op jit(solution)/shard_map/dot_general | solution.py:38
  334.3 92.8 %all-reduce.16.cloned.1.call-done = f32[3584,128]{1,0:T(8,128)} async-done(((f32[3584,128]{1,0:T(8,128)}), f32[3584,128]{1,0:T(8,128)}) %all-reduce.16.cloned.1.call-update) | async-done | bytes 1835024 | tf_op jit(solution)/shard_map/psum | solution.py:39
  427.1 1.7 fusion.2
  429.7 5.1 convolution_bitcast_fusion.2
  439.0 1.7 fusion.10
  440.7 41.8 %all-reduce = (f32[]{:T(128)}, f32[]{:T(128)}, f32[]{:T(128)}, f32[]{:T(128)}, f32[]{:T(128)}, /*index=5*/f32[]{:T(128)}, f32[]{:T(128)}, f32[]{:T(128)}, f32[]{:T(128)}, f32[1]{0:T(128)}, /*index=10*/f32[1]{0:T(128)}) all-reduce(f32[]{:T(128)} %get-tuple-element.12, ...), channel_id=1, replica_groups=mesh['feat'=8,'samp'=4] {'feat','samp'}, use_global_device_ids=true, to_apply=%region_38.0 | all-reduce | flops 11 | bytes 88 | tf_op jit(solution)/shard_map/psum | solution.py:56
  486.2 1.9 pad_maximum_fusion.2
  489.9 21.7 %all-reduce.1 = (f32[]{:T(128)}, f32[]{:T(128)}, f32[]{:T(128)}) all-reduce(f32[]{:T(128)} %sqrt_reduce_fusion.4, f32[]{:T(128)} %sqrt_reduce_fusion.5, f32[]{:T(128)} %sqrt_reduce_fusion.6), channel_id=1, replica_groups=mesh['feat'=8,'samp'=4] {'feat'}, use_global_device_ids=true, to_apply=%region_22.0 | all-reduce | flops 3 | bytes 24 | tf_op jit(solution)/shard_map/pmax | solution.py:55
  (49 shorter events, 14.8 us)
Async XLA Ops:
  7.2 6.6 %copy-start = (bf16[3584,128]{1,0:T(8,128)(2,1)S(1)}, bf16[3584,128]{1,0:T(8,128)(2,1)}, u32[]{:S(2)}) copy-start(bf16[3584,128]{1,0:T(8,128)(2,1)} %param.6) | copy-start | bytes 2752516
  7.2 105.3 %all-reduce.10.cloned.1.call-start = ((), (), s32[]{:S(2)}) async-start(), calls=%async_computation | async-start | bytes 3670016 | tf_op jit(solution)/shard_map/psum | solution.py:39
  13.7 141.5 %all-reduce.20.cloned.1.call-start = ((), (), s32[]{:S(2)}) async-start(), calls=%async_computation.5 | async-start | bytes 2097152 | tf_op jit(solution)/shard_map/psum | solution.py:52
  119.2 4.7 copy-start.4
  119.2 13.5 %copy-start.6 = (s32[2,1024]{1,0:T(2,128)S(1)}, s32[2,1024]{1,0:T(2,128)}, u32[]{:S(2)}) copy-start(s32[2,1024]{1,0:T(2,128)} %param.8) | copy-start | bytes 24580
  119.2 161.7 %all-reduce.12.cloned.1.call-start = ((), (), s32[]{:S(2)}) async-start(), calls=%async_computation.1 | async-start | bytes 3670016 | tf_op jit(solution)/shard_map/psum | solution.py:39
  188.1 132.6 %all-reduce.14.cloned.1.call-start = ((), (), s32[]{:S(2)}) async-start(), calls=%async_computation.2 | async-start | bytes 1048576 | tf_op jit(solution)/shard_map/psum | solution.py:52
  287.6 139.5 %all-reduce.16.cloned.1.call-start = ((), (), s32[]{:S(2)}) async-start(), calls=%async_computation.3 | async-start | bytes 3670016 | tf_op jit(solution)/shard_map/psum | solution.py:39
  323.7 0.8 copy-start.2
  323.8 7.3 %copy-start.5 = (f32[1024,128]{1,0:T(8,128)S(1)}, f32[1024,128]{1,0:T(8,128)}, u32[]{:S(2)}) copy-start(f32[1024,128]{1,0:T(8,128)} %param.7) | copy-start | bytes 1572868
  331.0 157.1 %all-reduce.18.cloned.1.call-start = ((), (), s32[]{:S(2)}) async-start(), calls=%async_computation.4 | async-start | bytes 1048576 | tf_op jit(solution)/shard_map/psum | solution.py:52
  428.7 0.9 copy-start.1
  429.7 5.8 %copy-start.3 = (f32[1024,128]{0,1:T(8,128)S(1)}, f32[1024,128]{0,1:T(8,128)}, u32[]{:S(2)}) copy-start(f32[1024,128]{0,1:T(8,128)} %copy-done.2) | copy-start | bytes 1572868
Sparse Core Ops, SparseCore 0:
  13.9 98.5 all-reduce.9
  119.3 35.8 all-reduce.19
  188.2 92.6 all-reduce.11
  287.7 32.9 all-reduce.13
  331.1 95.9 all-reduce.15
  434.9 33.1 all-reduce.17
where the time goes:
time: 528 us; the launch traced here: 527 us
  waiting for transfers between devices  334 us (63%)
  blocking collectives  92.5 us (18%)
  matrix products  40.5 us (8%)
  between operations  30.1 us (6%)
  other arithmetic  26.4 us (5%)
    psum x3, waiting for transfers between devices, local(): fitted = lax.psum(fitted_part, 'feat')  278 us
    psum x3, waiting for transfers between devices, local(): gradient = lax.psum(grad_local, 'samp')  55.4 us
    psum x1, blocking collectives, local(): lax.psum((rr_local, ry_local, bn_local, pruned_local), ('feat', 'samp'))  41.8 us
    pmax x1, blocking collectives, local(): penalty_max = lax.pmax(jnp.max(group_norms(corr_y)), 'feat')  22 us
    pmax x1, blocking collectives, local(): grad_top = lax.pmax(local_max, 'feat')  21.7 us
    dot_general x4, matrix products, transpose_product(): lax.dot_general(design, right_side, (((0,), (0,)), ((), ())), preferred_e...  21.2 us
    dot_general x3, matrix products, local(): jnp.dot(design, current_half, preferred_element_type=jnp.float32)  19.3 us
  transfers between devices with their start and end apart: 6, of which 5 were waited for; matrix products, arithmetic and copies ran while one was open for 4% of the time, Pallas kernels for 0%

commit v1 on v0

--- a/solution.py
+++ b/solution.py
@@ -36,7 +36,7 @@
     for iteration in range(ITERS + 1):
         current_half = current.astype(jnp.bfloat16)
         fitted_part = jnp.dot(design, current_half, preferred_element_type=jnp.float32)
-        fitted = lax.psum(fitted_part, "feat")
+        fitted = jnp.sum(lax.all_gather(fitted_part, "feat"), axis=0)
         residual_all = (targets.astype(jnp.float32) - fitted).astype(jnp.bfloat16)
         residual = lax.dynamic_slice_in_dim(residual_all, feat_slot * block_rows, block_rows, 0)
         grad_local = transpose_product(design, residual_all)

time: 528 us -> 927 us (1.76)
  waiting for transfers between devices: 334 us -> 650 us
  local copies, waits for them, and re-layouts: 3.71 us -> 52 us
  other arithmetic: 26.4 us -> 53.5 us
    all_gather x0 -> x3, waiting for transfers between devices: none -> 595 us  [local(): fitted = jnp.sum(lax.all_gather(fitted_part, 'feat'), axis=0)]
    psum x3 -> x0, waiting for transfers between devices: 278 us -> none  [local(): fitted = lax.psum(fitted_part, 'feat')]
    unnamed x16 -> x18, local copies, waits for them, and re-layouts: 3.71 us -> 46.5 us
    reduce_sum x0 -> x3, other arithmetic: none -> 27.3 us  [local(): fitted = jnp.sum(lax.all_gather(fitted_part, 'feat'), axis=0)]
  transfers between devices with their start and end apart: 6 -> 6, of which waited for: 5 -> 5; matrix products, arithmetic and copies ran while one was open for 4% -> 2% of each run, Pallas kernels for 0% -> 0%
where the time goes in v1:
time: 927 us; the launch traced here: 918 us
  waiting for transfers between devices  650 us (70%)
  blocking collectives  90.5 us (10%)
  other arithmetic  53.5 us (6%)
  local copies, waits for them, and re-layouts  52 us (6%)
  matrix products  41.4 us (4%)
  between operations  30.4 us (3%)
    all_gather x3, waiting for transfers between devices, local(): fitted = jnp.sum(lax.all_gather(fitted_part, 'feat'), axis=0)  595 us
    psum x3, waiting for transfers between devices, local(): gradient = lax.psum(grad_local, 'samp')  54.4 us
    unnamed x18, local copies, waits for them, and re-layouts  46.5 us
    psum x1, blocking collectives, local(): lax.psum((rr_local, ry_local, bn_local, pruned_local), ('feat', 'samp'))  40 us
    reduce_sum x3, other arithmetic, local(): fitted = jnp.sum(lax.all_gather(fitted_part, 'feat'), axis=0)  27.3 us
    pmax x1, blocking collectives, local(): grad_top = lax.pmax(local_max, 'feat')  22.1 us
    pmax x1, blocking collectives, local(): penalty_max = lax.pmax(jnp.max(group_norms(corr_y)), 'feat')  22 us
    dot_general x4, matrix products, transpose_product(): lax.dot_general(design, right_side, (((0,), (0,)), ((), ())), preferred_e...  21.2 us
  transfers between devices with their start and end apart: 6, of which 5 were waited for; matrix products, arithmetic and copies ran while one was open for 2% of the time, Pallas kernels for 0%

profile of v1, /device:TPU:0, one launch (start us, length us, event | category | flops | bytes accessed | tf_op | source)
XLA Modules:
  0.0 918.1 jit_solution(11315641028761405603)
XLA Ops:
  7.2 6.5 fusion.5
  13.8 6.0 fusion.13
  19.8 198.5 %all-gather.7.cloned.1.call-done = f32[28672,128]{1,0:T(8,128)} async-done(((f32[3584,128]{1,0:T(8,128)}), f32[28672,128]{1,0:T(8,128)}) %all-gather.7.cloned.1.call-update) | async-done | bytes 14680080 | tf_op jit(solution)/shard_map/all_gather | solution.py:39
  218.3 7.3 reduce_sum.217
  227.3 5.0 convolution_bitcast_fusion.4
  232.4 4.6 multiply_reduce_fusion
  237.9 6.4 psum.112
  244.4 22.7 %all-reduce.11.cloned.1.call-done = (f32[1024,128]{0,1:T(8,128)}, f32[1024,128]{1,0:T(8,128)}) async-done(((f32[1024,128]{0,1:T(8,128)}, f32[1024,128]{1,0:T(8,128)}), (f32[1024,128]{0,1:T(8,128)}, f32[1024,128]{1,0:T(8,128)})) %all-reduce.11.cloned.1.call-update) | async-done | bytes 1048592 | tf_op jit(solution)/shard_map/psum | solution.py:52
  269.0 22.0 %pmax.28 = f32[]{:T(128)} all-reduce(f32[]{:T(128)} %sqrt_reduce_fusion.3), channel_id=1, replica_groups=mesh['feat'=8,'samp'=4] {'feat'}, use_global_device_ids=true, to_apply=%region_8.0 | all-reduce | flops 1 | bytes 8 | tf_op jit(solution)/shard_map/pmax | solution.py:28
  293.4 6.9 convolution_bitcast_fusion.1
  300.5 198.4 %all-gather.9.cloned.1.call-done = f32[28672,128]{0,1:T(8,128)} async-done(((f32[3584,128]{0,1:T(8,128)}), f32[28672,128]{0,1:T(8,128)}) %all-gather.9.cloned.1.call-update) | async-done | bytes 14680080 | tf_op jit(solution)/shard_map/all_gather | solution.py:39
  498.9 21.7 %copy.19 = f32[16,8,8,3584]{3,2,1,0:T(8,128)} copy(f32[16,8,8,3584]{3,1,2,0:T(8,128)} %bitcast.44) | data formatting | bytes 29360128
  520.6 10.1 %bitcast_reduce_fusion.1 = f32[3584,128]{0,1:T(8,128)} fusion(f32[16,8,8,3584]{3,2,1,0:T(8,128)} %copy.19), kind=kLoop, calls=%fused_computation.1 | loop fusion | flops 3211264 | bytes 16515072 | tf_op jit(solution)/shard_map/reduce_sum | solution.py:39
  530.7 2.7 copy.16
  535.1 5.0 convolution_bitcast_fusion.3
  540.2 31.7 %all-reduce.7.cloned.1.call-done = f32[1024,128]{0,1:T(8,128)} async-done(((f32[1024,128]{0,1:T(8,128)}), f32[1024,128]{0,1:T(8,128)}) %all-reduce.7.cloned.1.call-update) | async-done | bytes 524304 | tf_op jit(solution)/shard_map/psum | solution.py:52
  575.7 6.8 convolution_bitcast_fusion
  586.4 198.1 %all-gather.11.cloned.1.call-done = f32[28672,128]{0,1:T(8,128)} async-done(((f32[3584,128]{0,1:T(8,128)}), f32[28672,128]{0,1:T(8,128)}) %all-gather.11.cloned.1.call-update) | async-done | bytes 14680080 | tf_op jit(solution)/shard_map/all_gather | solution.py:39
  784.5 21.9 %copy.20 = f32[16,8,8,3584]{3,2,1,0:T(8,128)} copy(f32[16,8,8,3584]{3,1,2,0:T(8,128)} %bitcast.43) | data formatting | bytes 29360128
  806.4 9.9 %bitcast_reduce_fusion = f32[3584,128]{0,1:T(8,128)} fusion(f32[16,8,8,3584]{3,2,1,0:T(8,128)} %copy.20), kind=kLoop, calls=%fused_computation | loop fusion | flops 3211264 | bytes 16515072 | tf_op jit(solution)/shard_map/reduce_sum | solution.py:39
  816.3 2.7 copy.17
  821.6 5.1 convolution_bitcast_fusion.2
  832.7 40.0 %all-reduce = (f32[]{:T(128)}, f32[]{:T(128)}, f32[]{:T(128)}, f32[]{:T(128)}, f32[]{:T(128)}, /*index=5*/f32[]{:T(128)}, f32[]{:T(128)}, f32[]{:T(128)}, f32[]{:T(128)}, f32[1]{0:T(128)}, /*index=10*/f32[1]{0:T(128)}) all-reduce(f32[]{:T(128)} %get-tuple-element.20, ...), channel_id=1, replica_groups=mesh['feat'=8,'samp'=4] {'feat','samp'}, use_global_device_ids=true, to_apply=%region_38.0 | all-reduce | flops 11 | bytes 88 | tf_op jit(solution)/shard_map/psum | solution.py:56
  880.1 22.1 %all-reduce.1 = (f32[]{:T(128)}, f32[]{:T(128)}, f32[]{:T(128)}) all-reduce(f32[]{:T(128)} %sqrt_reduce_fusion.4, f32[]{:T(128)} %sqrt_reduce_fusion.5, f32[]{:T(128)} %sqrt_reduce_fusion.6), channel_id=1, replica_groups=mesh['feat'=8,'samp'=4] {'feat'}, use_global_device_ids=true, to_apply=%region_22.0 | all-reduce | flops 3 | bytes 24 | tf_op jit(solution)/shard_map/pmax | solution.py:55
  (56 shorter events, 25.5 us)
Async XLA Ops:
  7.2 6.7 copy-start
  7.2 211.1 %all-gather.7.cloned.1.call-start = ((), (), s32[]{:S(2)}) async-start(), calls=%async_computation.2 | async-start | bytes 16515072 | tf_op jit(solution)/shard_map/all_gather | solution.py:39
  13.8 253.3 %all-reduce.11.cloned.1.call-start = ((), (), s32[]{:S(2)}) async-start(), calls=%async_computation.5 | async-start | bytes 2097152 | tf_op jit(solution)/shard_map/psum | solution.py:52
  232.4 4.7 copy-start.4
  232.4 12.0 %copy-start.6 = (s32[2,1024]{1,0:T(2,128)S(1)}, s32[2,1024]{1,0:T(2,128)}, u32[]{:S(2)}) copy-start(s32[2,1024]{1,0:T(2,128)} %param.8) | copy-start | bytes 24580
  232.4 266.5 %all-gather.9.cloned.1.call-start = ((), (), s32[]{:S(2)}) async-start(), calls=%async_computation.3 | async-start | bytes 16515072 | tf_op jit(solution)/shard_map/all_gather | solution.py:39
  300.3 271.6 %all-reduce.7.cloned.1.call-start = ((), (), s32[]{:S(2)}) async-start(), calls=%async_computation | async-start | bytes 1048576 | tf_op jit(solution)/shard_map/psum | solution.py:52
  540.2 244.4 %all-gather.11.cloned.1.call-start = ((), (), s32[]{:S(2)}) async-start(), calls=%async_computation.4 | async-start | bytes 16515072 | tf_op jit(solution)/shard_map/all_gather | solution.py:39
  574.9 0.8 copy-start.2
  574.9 8.1 copy-start.5
  582.6 295.8 %all-reduce.9.cloned.1.call-start = ((), (), s32[]{:S(2)}) async-start(), calls=%async_computation.1 | async-start | bytes 1048576 | tf_op jit(solution)/shard_map/psum | solution.py:52
  820.7 0.9 copy-start.1
  821.6 5.8 copy-start.3
Sparse Core Ops, SparseCore 0:
  13.9 204.3 all-gather.6
  232.5 34.5 all-reduce.10
  300.4 198.4 all-gather.8
  540.3 31.5 all-reduce.6
  582.7 201.7 all-gather.10
  826.9 31.6 all-reduce.8
